TPU v7x, 256 devices: a 2x2x32 block of a 4x8x32 slice. The times are simulated.
256 devices in a mesh: groups: 4 (over y, x), feat: 64 (over z, core).
Axes of the slice: x: 2, y: 2, z: 32, core: 2. Of those that a mesh axis runs over, the one named last changes fastest.
The devices are a block of a 4x8x32 slice.
Arguments:
- design: float32 [2048, 131072], P('groups', 'feat'), parts along dimension 0, may hold values from -6 to 6
- targets: float32 [2048, 128], P('groups'), parts along dimension 0, may hold values from -6 to 6
- coef_now: float32 [524288, 128], P(('groups', 'feat')), parts along dimension 0, may hold values from -1 to 1
- coef_prev: float32 [524288, 128], P(('groups', 'feat')), parts along dimension 0, may hold values from -1 to 1
- penalty: float32 [512], P('groups'), parts along dimension 0, may hold values from 0.1 to 1
- drop_mask: int32 [4096], P(('groups', 'feat')), parts along dimension 0, may hold values from 0 to 1, as said below
- dest_shard: int32 [4096], P(('groups', 'feat')), parts along dimension 0, may hold values from 0 to 63, as said below
Outputs:
- coef_out: float32 [786432, 128], P(('groups', 'feat')), parts along dimension 0
- design_out: float32 [2048, 196608], P('groups', 'feat'), parts along dimension 0
- duality_gap: float32 [512], P('groups'), parts along dimension 0
- dual_value: float32 [512], P('groups'), parts along dimension 0
- coef_l1: float32 [512], P('groups'), parts along dimension 0
There are 4 independent parts, one for each index of `groups`. A program takes and returns all parts, laid end to end along the dimension named above; each array names one. Nothing has to cross between parts.
Inputs may be any that keep to these rules, and one draw needn't show every extreme that they name: `drop_mask`: screening marks blocks to drop with 1; shards drop very different shares of their blocks. `dest_shard`: a block's destination is its own shard, except that any of the first 4 blocks of a shard may go to the shard before it (cyclically) and any of the last 4 blocks to the shard after it; no shard receives more than 24 surviving blocks, and some shard receives exactly 24 in every draw.
All inputs are finite; a program needn't handle non-finite values.
Results may differ from a plain program's by a relative error of at most 0.0003.
Values sent between devices are 32-bit elements; how exact they have to be, the bound alone decides.
A program may use at most 64 MiB of HBM per device.

v0:
```python
import math

import jax
import jax.numpy as jnp
from jax import lax
from jax.sharding import PartitionSpec as P

START = 40


precise = lax.Precision.HIGHEST


def shifted(value, axis, steps):
    count = lax.axis_size(axis)
    pairs = [(source, (source + steps) % count) for source in range(count)]
    return lax.ppermute(value, axis, pairs)


def split_up(shard, dim, size):
    shape = shard.shape
    blocks = shard.reshape(*shape[:dim], size, shape[dim] // size, *shape[dim + 1 :])
    return jnp.moveaxis(blocks, dim, 0)


def sent_and_summed(shard, axis, dim):
    size = lax.axis_size(axis)
    blocks = lax.all_to_all(split_up(shard, dim, size), axis, 0, 0, tiled=True)
    return jnp.sum(blocks, axis=0)


def joined_along(blocks, dim):
    blocks = jnp.moveaxis(blocks, 0, dim)
    shape = blocks.shape
    return blocks.reshape(*shape[:dim], shape[dim] * shape[dim + 1], *shape[dim + 2 :])


def copy_for_each(shard, axis):
    copies = jnp.broadcast_to(shard, (lax.axis_size(axis), *shard.shape))
    return lax.all_to_all(copies, axis, split_axis=0, concat_axis=0, tiled=True)


def collect(shard, axis, dim):
    return joined_along(copy_for_each(shard, axis), dim)


def of_everyone(shard, axis):
    return copy_for_each(shard, axis).max(axis=0)


def over_copies(shard, axis):
    return copy_for_each(shard, axis).sum(axis=0)


def shrink(values, level):
    return jnp.sign(values) * jnp.maximum(jnp.abs(values) - level, 0.0)


def local(design, targets, coef_now, coef_prev, penalty, drop_mask, dest_shard):
    sample_count, local_feats = design.shape
    shards = lax.axis_size("feat")
    my_index = lax.axis_index("feat")
    lipschitz = (math.sqrt(sample_count) + math.sqrt(local_feats * shards)) ** 2
    level = penalty * (sample_count / lipschitz)
    first_push = (START - 1) / (START + 2)
    second_push = START / (START + 3)
    block_count = local_feats // 128
    edge_count = block_count // 4
    survive = drop_mask == 0
    to_left = survive[:edge_count] & (dest_shard[:edge_count] == (my_index + shards - 1) % shards)
    to_right = survive[block_count - edge_count :] & (
        dest_shard[block_count - edge_count :] == (my_index + 1) % shards
    )
    staying = survive & (dest_shard == my_index)
    left_flags = to_left.astype(jnp.int32)
    right_flags = to_right.astype(jnp.int32)
    design_blocks = design.reshape(sample_count, block_count, 128)
    left_design = design_blocks[:, :edge_count]
    right_design = design_blocks[:, block_count - edge_count :]
    before_design, before_flags = shifted((right_design, right_flags), "feat", 1)
    after_design, after_flags = shifted((left_design, left_flags), "feat", -1)

    def misfit_of(point):
        row_count = sample_count // shards
        fitted_rows = sent_and_summed(
            jnp.dot(design, point, precision=precise, preferred_element_type=jnp.float32), "feat", 0
        )
        own_targets = lax.dynamic_slice_in_dim(targets, my_index * row_count, row_count, 0)
        misfit = collect(fitted_rows - own_targets, "feat", 0)
        return misfit

    def correlate(misfit):
        return lax.dot_general(
            design,
            misfit,
            (((0,), (0,)), ((), ())),
            precision=precise,
            preferred_element_type=jnp.float32,
        )

    def descend(point):
        misfit = misfit_of(point)
        return shrink(point - correlate(misfit) / lipschitz, level)

    coef_one = descend(coef_now + first_push * (coef_now - coef_prev))
    coef_two = descend(coef_one + second_push * (coef_one - coef_now))
    residual = -misfit_of(coef_two)
    correlation = correlate(residual)
    local_peak = jnp.max(jnp.abs(correlation), axis=0)
    local_mass = jnp.sum(jnp.abs(coef_two), axis=0)
    peak = of_everyone(local_peak, "feat")
    mass = over_copies(local_mass, "feat")
    dual_scale = jnp.maximum(penalty, peak / sample_count)
    dual_point = targets - penalty * residual / dual_scale
    dual_value = (jnp.sum(targets * targets, axis=0) - jnp.sum(dual_point * dual_point, axis=0)) / (
        2.0 * sample_count
    )
    primal = jnp.sum(residual * residual, axis=0) / (2.0 * sample_count) + penalty * mass
    duality_gap = primal - dual_value
    coef_blocks = coef_two.reshape(block_count, 128, coef_two.shape[1])
    left_coef = coef_blocks[:edge_count]
    right_coef = coef_blocks[block_count - edge_count :]
    before_coef = shifted(right_coef, "feat", 1)
    after_coef = shifted(left_coef, "feat", -1)
    arrived = jnp.concatenate([before_flags, staying.astype(jnp.int32), after_flags])
    slot_total = arrived.shape[0]
    slot_of = jnp.cumsum(arrived, dtype=jnp.int32) - 1
    placement = (
        (slot_of[:, None] == jnp.arange(slot_total, dtype=jnp.int32)[None, :])
        & (arrived[:, None] > 0)
    ).astype(jnp.float32)
    design_cands = jnp.concatenate([before_design, design_blocks, after_design], axis=1)
    design_out = jnp.einsum("ncf,cj->njf", design_cands, placement, precision=precise).reshape(
        sample_count, slot_total * 128
    )
    coef_cands = jnp.concatenate([before_coef, coef_blocks, after_coef], axis=0)
    coef_out = jnp.einsum("cfk,cj->jfk", coef_cands, placement, precision=precise).reshape(
        slot_total * 128, coef_two.shape[1]
    )
    return (coef_out, design_out, duality_gap, dual_value, mass)


def solution(mesh):
    placed = (
        P("groups", "feat"),
        P("groups", None),
        P(("groups", "feat"), None),
        P(("groups", "feat"), None),
        P("groups"),
        P(("groups", "feat")),
        P(("groups", "feat")),
    )
    return jax.shard_map(
        local,
        mesh=mesh,
        in_specs=placed,
        out_specs=(
            P(("groups", "feat"), None),
            P("groups", "feat"),
            P("groups"),
            P("groups"),
            P("groups"),
        ),
        check_vma=False,
    )
```

profile of v0, /device:TPU:37, one launch (start us, length us, event | category | flops | bytes accessed | tf_op | source)
XLA Modules:
  0.0 437.3 jit_solution(12467916481591101126)
XLA Ops:
  0.6 1.6 copy.46
  2.2 1.6 copy.47
  3.8 6.4 %convolution_bitcast_fusion.2 = f32[512,128]{0,1:T(8,128)S(1)} fusion(f32[512,2048]{1,0:T(8,128)} %param.7, f32[2048,128]{0,1:T(8,128)S(1)} %copy.47, f32[2048,128]{0,1:T(8,128)S(1)} %copy.46), kind=kOutput, calls=%fused_computation.23 | convolution fusion | flops 1611399168 | bytes 6553600 | tf_op jit(solution)/shard_map/dot_general | solution.py:86
  10.2 0.8 copy.48
  11.0 34.3 %all-to-all-start = ((f32[64,8,128]{2,1,0:T(8,128)}), f32[64,8,128]{2,1,0:T(8,128)S(1)}, u32[]{:S(2)}, u32[]{:S(2)}) async-start(f32[64,8,128]{2,1,0:T(8,128)} %bitcast.3), calls=%async_computation | async-start | bytes 524288 | tf_op jit(solution)/shard_map/all_to_all | solution.py:28
  45.4 41.1 %all-to-all-done = f32[64,8,128]{2,1,0:T(8,128)S(1)} async-done(((f32[64,8,128]{2,1,0:T(8,128)}), f32[64,8,128]{2,1,0:T(8,128)S(1)}, u32[]{:S(2)}, u32[]{:S(2)}) %all-to-all-start) | async-done | bytes 262176 | tf_op jit(solution)/shard_map/all_to_all | solution.py:28
  86.6 0.7 dynamic-slice_subtract_fusion.2
  87.3 0.7 broadcast_in_dim.10
  88.0 7.3 %all-to-all-start.1 = ((f32[64,8,128]{2,1,0:T(8,128)}), f32[64,8,128]{2,1,0:T(8,128)S(1)}, u32[]{:S(2)}, u32[]{:S(2)}) async-start(f32[64,8,128]{2,1,0:T(8,128)} %broadcast_in_dim.10), calls=%async_computation.1 | async-start | bytes 524288 | tf_op jit(solution)/shard_map/all_to_all | solution.py:40
  95.4 41.3 %all-to-all-done.1 = f32[64,8,128]{2,1,0:T(8,128)S(1)} async-done(((f32[64,8,128]{2,1,0:T(8,128)}), f32[64,8,128]{2,1,0:T(8,128)S(1)}, u32[]{:S(2)}, u32[]{:S(2)}) %all-to-all-start.1) | async-done | bytes 262176 | tf_op jit(solution)/shard_map/all_to_all | solution.py:40
  136.6 5.2 %multiply_add_fusion = f32[2048,128]{0,1:T(8,128)S(1)} fusion(f32[2048,128]{0,1:T(8,128)S(1)} %copy.47, f32[512,2048]{1,0:T(8,128)} %param.7, f32[2048,128]{0,1:T(8,128)S(1)} %copy.46, f32[128]{0:T(128)S(1)} %broadcast_multiply_fusion, f32[64,8,128]{2,1,0:T(8,128)S(1)} %all-to-all-done.1), kind=kOutput, calls=%fused_computation.26 | convolution fusion | flops 1614020608 | bytes 7602688 | tf_op jit(solution)/shard_map/dot_general | solution.py:93
  141.9 4.5 %convolution_bitcast_fusion.1 = f32[512,128]{0,1:T(8,128)S(1)} fusion(f32[2048,128]{0,1:T(8,128)S(1)} %multiply_add_fusion, f32[512,2048]{1,0:T(8,128)S(1)} %copy-done), kind=kOutput, calls=%fused_computation.22 | convolution fusion | flops 1610612736 | bytes 5505024 | tf_op jit(solution)/shard_map/dot_general | solution.py:86
  146.4 0.1 copy.50
  146.5 48.4 %all_to_all.42 = f32[64,8,128]{2,1,0:T(8,128)S(1)} all-to-all(f32[64,8,128]{2,1,0:T(8,128)S(1)} %bitcast.80), channel_id=1, replica_groups=mesh['groups'=4,'feat'=64] {'feat'}, dimensions={0} | all-to-all | bytes 524288 | tf_op jit(solution)/shard_map/all_to_all | solution.py:28
  194.9 0.8 dynamic-slice_subtract_fusion.1
  195.8 47.3 %all_to_all.43 = f32[64,8,128]{2,1,0:T(8,128)S(1)} all-to-all(f32[64,8,128]{2,1,0:T(8,128)S(1)} %broadcast_in_dim.11), channel_id=1, replica_groups=mesh['groups'=4,'feat'=64] {'feat'}, dimensions={0} | all-to-all | bytes 524288 | tf_op jit(solution)/shard_map/all_to_all | solution.py:40
  243.1 5.0 %abs_reduce_fusion = (f32[128]{0:T(128)S(1)}, f32[2048,128]{0,1:T(8,128)S(1)}) fusion(f32[128]{0:T(128)S(1)} %broadcast_multiply_fusion, f32[2048,128]{0,1:T(8,128)S(1)} %multiply_add_fusion, f32[512,2048]{1,0:T(8,128)} %param.7, f32[64,8,128]{2,1,0:T(8,128)S(1)} %all_to_all.43), kind=kOutput, calls=%fused_computation.24 | convolution fusion | flops 1612971904 | bytes 6554624 | tf_op jit(solution)/shard_map/dot_general | solution.py:93
  248.1 4.5 %convolution_bitcast_fusion = f32[512,128]{0,1:T(8,128)S(1)} fusion(f32[2048,128]{0,1:T(8,128)S(1)} %get-tuple-element.20, f32[512,2048]{1,0:T(8,128)S(1)} %copy-done.1), kind=kOutput, calls=%fused_computation.21 | convolution fusion | flops 1610612736 | bytes 5505024 | tf_op jit(solution)/shard_map/dot_general | solution.py:86
  252.7 47.9 %all_to_all.44 = f32[64,8,128]{2,1,0:T(8,128)S(1)} all-to-all(f32[64,8,128]{2,1,0:T(8,128)S(1)} %bitcast.81), channel_id=1, replica_groups=mesh['groups'=4,'feat'=64] {'feat'}, dimensions={0} | all-to-all | bytes 524288 | tf_op jit(solution)/shard_map/all_to_all | solution.py:28
  300.6 0.6 broadcast_in_dim.25
  301.3 5.5 %all-to-all-start.6 = ((f32[64,1,128]{2,1,0:T(1,128)}), f32[64,1,128]{2,1,0:T(1,128)S(1)}, u32[]{:S(2)}, u32[]{:S(2)}) async-start(f32[64,1,128]{2,1,0:T(1,128)} %broadcast_in_dim.25), calls=%async_computation.6 | async-start | bytes 65536 | tf_op jit(solution)/shard_map/all_to_all | solution.py:40
  306.9 0.7 dynamic-slice_subtract_fusion
  307.6 21.7 %all-to-all-done.6 = f32[64,1,128]{2,1,0:T(1,128)S(1)} async-done(((f32[64,1,128]{2,1,0:T(1,128)}), f32[64,1,128]{2,1,0:T(1,128)S(1)}, u32[]{:S(2)}, u32[]{:S(2)}) %all-to-all-start.6) | async-done | bytes 32800 | tf_op jit(solution)/shard_map/all_to_all | solution.py:40
  329.3 0.7 broadcast_in_dim.24
  330.1 6.6 %all-to-all-start.5 = ((f32[64,8,128]{2,1,0:T(8,128)}), f32[64,8,128]{2,1,0:T(8,128)S(1)}, u32[]{:S(2)}, u32[]{:S(2)}) async-start(f32[64,8,128]{2,1,0:T(8,128)} %broadcast_in_dim.24), calls=%async_computation.5 | async-start | bytes 524288 | tf_op jit(solution)/shard_map/all_to_all | solution.py:40
  336.6 3.1 copy.59
  339.8 2.0 copy-done.2
  341.8 1.7 fusion.37
  343.5 1.7 collective-permute-start.4
  345.2 1.7 collective-permute-start
  346.9 0.9 collective-permute-start.1
  347.8 23.1 %collective-permute-done = s32[4]{0:T(128)S(1)} collective-permute-done((s32[4]{0:T(128)S(1)}, s32[4]{0:T(128)S(1)}, u32[]{:S(2)}, u32[]{:S(2)}) %collective-permute-start) | collective-permute-done | bytes 48 | tf_op jit(solution)/shard_map/ppermute | solution.py:17
  370.9 0.8 collective-permute-done.1
  372.0 6.2 %fusion = f32[24,512,128]{2,0,1:T(8,128)S(1)} fusion(f32[512,4,128]{2,1,0:T(4,128)S(1)} %collective-permute-done.5, f32[512,16,128]{2,1,0:T(8,128)} %bitcast.74, f32[512,4,128]{2,1,0:T(4,128)S(1)} %collective-permute-done.4, s32[24]{0:T(128)S(1)} %add_reduce_fusion, pred[24]{0:T(512)(128)(4,1)S(1)} %get-tuple-element.9), kind=kOutput, calls=%fused_computation.1 | convolution fusion | flops 456131712 | bytes 12583032 | tf_op jit(solution)/shard_map/ncf,cj->njf/dot_general | solution.py:133
  378.2 4.1 copy.62
  382.4 0.2 copy.51
  382.6 1.7 collective-permute-start.2
  384.4 0.2 copy.52
  384.5 1.2 collective-permute-start.3
  385.8 0.2 copy.58
  386.0 0.7 copy.53
  386.7 4.6 %fusion.16 = f32[128]{0:T(128)S(1)} fusion(f32[512,2048]{1,0:T(8,128)} %param.7, f32[64,8,128]{2,1,0:T(8,128)S(1)} %all-to-all-done.5), kind=kOutput, calls=%fused_computation.20 | convolution fusion | flops 1611202432 | bytes 4456960 | tf_op jit(solution)/shard_map/dot_general | solution.py:93
  391.3 0.6 broadcast_in_dim.26
  392.0 22.5 %all-to-all-start.7 = ((f32[64,1,128]{2,1,0:T(1,128)}), f32[64,1,128]{2,1,0:T(1,128)S(1)}, u32[]{:S(2)}, u32[]{:S(2)}) async-start(f32[64,1,128]{2,1,0:T(1,128)} %broadcast_in_dim.26), calls=%async_computation.7 | async-start | bytes 65536 | tf_op jit(solution)/shard_map/all_to_all | solution.py:40
  414.4 1.0 fusion.10
  415.5 1.4 copy.54
  417.0 19.5 %all-to-all-done.7 = f32[64,1,128]{2,1,0:T(1,128)S(1)} async-done(((f32[64,1,128]{2,1,0:T(1,128)}), f32[64,1,128]{2,1,0:T(1,128)S(1)}, u32[]{:S(2)}, u32[]{:S(2)}) %all-to-all-start.7) | async-done | bytes 32800 | tf_op jit(solution)/shard_map/all_to_all | solution.py:40
  436.6 0.5 add_subtract_fusion
  (41 shorter events, 1.3 us)
Async XLA Ops:
  3.8 91.6 %copy-start.6 = (f32[128]{0:T(128)S(1)}, f32[128]{0:T(128)}, u32[]{:S(2)}) copy-start(f32[128]{0:T(128)} %param.11) | copy-start | bytes 1540
  11.0 75.5 %all-to-all-start = ((f32[64,8,128]{2,1,0:T(8,128)}), f32[64,8,128]{2,1,0:T(8,128)S(1)}, u32[]{:S(2)}, u32[]{:S(2)}) async-start(f32[64,8,128]{2,1,0:T(8,128)} %bitcast.3), calls=%async_computation | async-start | bytes 524288 | tf_op jit(solution)/shard_map/all_to_all | solution.py:28
  88.0 48.6 %all-to-all-start.1 = ((f32[64,8,128]{2,1,0:T(8,128)}), f32[64,8,128]{2,1,0:T(8,128)S(1)}, u32[]{:S(2)}, u32[]{:S(2)}) async-start(f32[64,8,128]{2,1,0:T(8,128)} %broadcast_in_dim.10), calls=%async_computation.1 | async-start | bytes 524288 | tf_op jit(solution)/shard_map/all_to_all | solution.py:40
  136.6 5.2 %copy-start = (f32[512,2048]{1,0:T(8,128)S(1)}, f32[512,2048]{1,0:T(8,128)}, u32[]{:S(2)}) copy-start(f32[512,2048]{1,0:T(8,128)} %param.7) | copy-start | bytes 12582916
  194.9 53.2 %copy-start.1 = (f32[512,2048]{1,0:T(8,128)S(1)}, f32[512,2048]{1,0:T(8,128)}, u32[]{:S(2)}) copy-start(f32[512,2048]{1,0:T(8,128)} %param.7) | copy-start | bytes 12582916
  301.3 28.1 %all-to-all-start.6 = ((f32[64,1,128]{2,1,0:T(1,128)}), f32[64,1,128]{2,1,0:T(1,128)S(1)}, u32[]{:S(2)}, u32[]{:S(2)}) async-start(f32[64,1,128]{2,1,0:T(1,128)} %broadcast_in_dim.25), calls=%async_computation.6 | async-start | bytes 65536 | tf_op jit(solution)/shard_map/all_to_all | solution.py:40
  330.1 56.6 %all-to-all-start.5 = ((f32[64,8,128]{2,1,0:T(8,128)}), f32[64,8,128]{2,1,0:T(8,128)S(1)}, u32[]{:S(2)}, u32[]{:S(2)}) async-start(f32[64,8,128]{2,1,0:T(8,128)} %broadcast_in_dim.24), calls=%async_computation.5 | async-start | bytes 524288 | tf_op jit(solution)/shard_map/all_to_all | solution.py:40
  339.7 2.0 copy-start.2
  339.8 5.4 %copy-start.4 = (s32[16]{0:T(128)S(1)}, s32[16]{0:T(128)}, u32[]{:S(2)}) copy-start(s32[16]{0:T(128)} %param.13) | copy-start | bytes 196
  339.8 5.3 %copy-start.7 = (s32[16]{0:T(128)S(1)}, s32[16]{0:T(128)}, u32[]{:S(2)}) copy-start(s32[16]{0:T(128)} %param.12) | copy-start | bytes 196
  343.5 28.5 %collective-permute-start.4 = (f32[512,4,128]{2,1,0:T(4,128)}, f32[512,4,128]{2,1,0:T(4,128)S(1)}, u32[]{:S(2)}, u32[]{:S(2)}) collective-permute-start(f32[512,4,128]{2,1,0:T(4,128)} %get-tuple-element.11), channel_id=1, source_target_pairs={{0,1},{1,2},{2,3},{3,4},{4,5},{5,6},{6,7},{7,8},{8,9},{9,10},{10,1... | collective-permute-start | bytes 3145736 | tf_op jit(solution)/shard_map/ppermute | solution.py:17
  345.1 26.9 %collective-permute-start.5 = (f32[512,4,128]{2,1,0:T(4,128)}, f32[512,4,128]{2,1,0:T(4,128)S(1)}, u32[]{:S(2)}, u32[]{:S(2)}) collective-permute-start(f32[512,4,128]{2,1,0:T(4,128)} %get-tuple-element.12), channel_id=1, source_target_pairs={{0,63},{1,0},{2,1},{3,2},{4,3},{5,4},{6,5},{7,6},{8,7},{9,8},{10,9... | collective-permute-start | bytes 3145736 | tf_op jit(solution)/shard_map/ppermute | solution.py:17
  345.2 25.7 %collective-permute-start = (s32[4]{0:T(128)S(1)}, s32[4]{0:T(128)S(1)}, u32[]{:S(2)}, u32[]{:S(2)}) collective-permute-start(s32[4]{0:T(128)S(1)} %get-tuple-element.15), channel_id=1, source_target_pairs={{0,1},{1,2},{2,3},{3,4},{4,5},{5,6},{6,7},{7,8},{8,9},{9,10},{10,1... | collective-permute-start | bytes 56 | tf_op jit(solution)/shard_map/ppermute | solution.py:17
  346.9 24.7 %collective-permute-start.1 = (s32[4]{0:T(128)S(1)}, s32[4]{0:T(128)S(1)}, u32[]{:S(2)}, u32[]{:S(2)}) collective-permute-start(s32[4]{0:T(128)S(1)} %get-tuple-element.16), channel_id=1, source_target_pairs={{0,63},{1,0},{2,1},{3,2},{4,3},{5,4},{6,5},{7,6},{8,7},{9,8},{10,9... | collective-permute-start | bytes 56 | tf_op jit(solution)/shard_map/ppermute | solution.py:17
  382.6 31.9 %collective-permute-start.2 = (f32[4,128,128]{2,0,1:T(4,128)S(1)}, f32[4,128,128]{2,0,1:T(4,128)S(1)}, u32[]{:S(2)}, u32[]{:S(2)}) collective-permute-start(f32[4,128,128]{2,0,1:T(4,128)S(1)} %copy.51), channel_id=1, source_target_pairs={{0,1},{1,2},{2,3},{3,4},{4,5},{5,6},{6,7},{7,8},{8,9},{9,10},{10,1... | collective-permute-start | bytes 786440 | tf_op jit(solution)/shard_map/ppermute | solution.py:17
  384.5 29.9 %collective-permute-start.3 = (f32[4,128,128]{2,0,1:T(4,128)S(1)}, f32[4,128,128]{2,0,1:T(4,128)S(1)}, u32[]{:S(2)}, u32[]{:S(2)}) collective-permute-start(f32[4,128,128]{2,0,1:T(4,128)S(1)} %copy.52), channel_id=1, source_target_pairs={{0,63},{1,0},{2,1},{3,2},{4,3},{5,4},{6,5},{7,6},{8,7},{9,8},{10,9... | collective-permute-start | bytes 786440 | tf_op jit(solution)/shard_map/ppermute | solution.py:17
  386.7 49.9 %copy-start.5 = (f32[128]{0:T(128)}, f32[128]{0:T(128)S(1)}, u32[]{:S(2)}) copy-start(f32[128]{0:T(128)S(1)} %reduce_sum.77) | copy-start | bytes 1540
  391.3 45.2 %copy-start.3 = (f32[512,128]{1,0:T(8,128)S(1)}, f32[512,128]{1,0:T(8,128)}, u32[]{:S(2)}) copy-start(f32[512,128]{1,0:T(8,128)} %param.8) | copy-start | bytes 786436
  392.0 44.5 %all-to-all-start.7 = ((f32[64,1,128]{2,1,0:T(1,128)}), f32[64,1,128]{2,1,0:T(1,128)S(1)}, u32[]{:S(2)}, u32[]{:S(2)}) async-start(f32[64,1,128]{2,1,0:T(1,128)} %broadcast_in_dim.26), calls=%async_computation.7 | async-start | bytes 65536 | tf_op jit(solution)/shard_map/all_to_all | solution.py:40
where the time goes:
time: 444 us; the launch traced here: 437 us
  waiting for transfers between devices  148 us (33%)
  blocking collectives  144 us (32%)
  starting transfers between devices  83.5 us (19%)
  matrix products  37.4 us (8%)
  local copies, waits for them, and re-layouts  20.7 us (5%)
    all_to_all x2, blocking collectives, sent_and_summed(): blocks = lax.all_to_all(split_up(shard, dim, size), axis, 0, 0, tiled=True)  96.3 us
    all_to_all x4, waiting for transfers between devices, copy_for_each(): return lax.all_to_all(copies, axis, split_axis=0, concat_axis=0, tiled=True)  82.5 us
    all_to_all x1, blocking collectives, copy_for_each(): return lax.all_to_all(copies, axis, split_axis=0, concat_axis=0, tiled=True)  47.3 us
    all_to_all x4, starting transfers between devices, copy_for_each(): return lax.all_to_all(copies, axis, split_axis=0, concat_axis=0, tiled=True)  41.9 us
    all_to_all x1, waiting for transfers between devices, sent_and_summed(): blocks = lax.all_to_all(split_up(shard, dim, size), axis, 0, 0, tiled=True)  41.1 us
    all_to_all x1, starting transfers between devices, sent_and_summed(): blocks = lax.all_to_all(split_up(shard, dim, size), axis, 0, 0, tiled=True)  34.3 us
    ppermute x6, waiting for transfers between devices, shifted(): return lax.ppermute(value, axis, pairs)  23.9 us
    dot_general x3, matrix products, misfit_of(): jnp.dot(design, point, precision=precise, preferred_element_type=jnp.floa...  15.4 us
  transfers between devices with their start and end apart: 11, of which 6 were waited for; matrix products, arithmetic and copies ran while one was open for 6% of the time, Pallas kernels for 0%

commit v1 on v0

v1 whole, which is shorter than its diff:
```python
import functools
import math

import jax
import jax.numpy as jnp
from jax import lax
from jax.experimental import pallas as pl
from jax.experimental.pallas import tpu as pltpu
from jax.sharding import PartitionSpec as P

START = 40
NEAR = 8
REACH = NEAR // 2
BLOCK = 128
CHUNKS = 4
MESH = pl.DeviceIdType.MESH
f32 = jnp.float32
bf16 = jnp.bfloat16


def at(device):
    return {"feat": device}


def halves(value):
    high = value.astype(bf16)
    return high, (value - high.astype(f32)).astype(bf16)


def fit_kernel(
    design, targets, now, prev, penalty, drop, dest,
    coef_home, edge_design, edge_coef, flags, stats,
    coef_two, raw, tgt, cur, old, pen, drop_in, dest_in, rows, cols, wide, point, corr,
    part, half, sent, near, own, far, total, misfit, mine, theirs, both, fin,
    load_sem, pair_send, pair_recv, near_send, near_recv, far_send, far_recv,
    all_send, all_recv, pass_send, pass_recv, edge_send, edge_recv, end_send, end_recv, word,
):
    samples, feats = raw.shape
    half_rows = samples // 2
    piece = half_rows // NEAR
    chunk = feats // CHUNKS
    devices = lax.axis_size("feat")
    chips = devices // 2
    blocks = chips // NEAR
    lipschitz = (math.sqrt(samples) + math.sqrt(feats * devices)) ** 2
    first_push = (START - 1) / (START + 2)
    second_push = START / (START + 3)
    edge = feats // 4
    me = lax.axis_index("feat")
    z = me // 2
    c = lax.rem(me, 2)
    partner = z * 2 + 1 - c
    after = lax.rem(me + 1, devices)
    before = lax.rem(me + devices - 1, devices)
    k = lax.rem(z, NEAR)
    block = z // NEAR

    def chip(d):
        return lax.rem(z + d + chips, chips)

    def same(d):
        return chip(d) * 2 + c

    barrier = pltpu.get_barrier_semaphore()

    def hello(semaphore, device):
        pl.semaphore_signal(semaphore, inc=1, device_id=at(device), device_id_type=MESH)

    for d in range(1, REACH + 1):
        hello(barrier, same(d))
        hello(barrier, same(-d))
    hello(barrier, before)
    hello(barrier, after)

    loads = [
        pltpu.make_async_copy(now, cur, load_sem.at[0]),
        pltpu.make_async_copy(prev, old, load_sem.at[1]),
    ]
    for i in range(CHUNKS):
        part_of = pl.ds(i * chunk, chunk)
        loads.append(pltpu.make_async_copy(design.at[:, part_of], raw.at[:, part_of], load_sem.at[2 + i]))
    for i, (source, target) in enumerate(((targets, tgt), (penalty, pen), (drop, drop_in), (dest, dest_in))):
        loads.append(pltpu.make_async_copy(source, target, load_sem.at[2 + CHUNKS + i]))
    for load in loads:
        load.start()

    def remote(source, target, send, recv, device):
        return pltpu.make_async_remote_copy(
            src_ref=source, dst_ref=target, send_sem=send, recv_sem=recv, device_id=at(device), device_id_type=MESH
        )

    def drain(ref, sem):
        pltpu.make_async_copy(ref, ref, sem).wait()

    def set_point(i, value):
        high, low = halves(value)
        here = pl.ds(i * chunk, chunk)
        wide[here, 0:BLOCK] = high
        wide[here, BLOCK : 2 * BLOCK] = low
        point[here, :] = value

    def fitted(h):
        both_parts = jnp.dot(rows[h], wide[...], preferred_element_type=f32)
        summed = both_parts[:half_rows] + both_parts[half_rows:]
        return summed[:, :BLOCK] + summed[:, BLOCK:]

    loads[0].wait()
    loads[1].wait()
    for i in range(CHUNKS):
        here = pl.ds(i * chunk, chunk)
        set_point(i, cur[here, :] + first_push * (cur[here, :] - old[here, :]))
    for i in range(CHUNKS):
        loads[2 + i].wait()
        here = pl.ds(i * chunk, chunk)
        for h in range(2):
            high, low = halves(raw[h * half_rows : (h + 1) * half_rows, here])
            rows[h, 0:half_rows, here] = high
            rows[h, half_rows : 2 * half_rows, here] = low
    for load in loads[2 + CHUNKS :]:
        load.wait()
    level = pen[...] * (samples / lipschitz)
    flags[0:8, :] = jnp.zeros((8, BLOCK), jnp.int32)
    flags[0:1, 0 : drop_in.shape[1]] = drop_in[...]
    flags[1:2, 0 : dest_in.shape[1]] = dest_in[...]

    def transpose_design():
        for h in range(2):
            for p in range(2):
                for i in range(CHUNKS):
                    tile = rows[h, p * half_rows : (p + 1) * half_rows, i * chunk : (i + 1) * chunk]
                    cols[h, i, p * chunk : (p + 1) * chunk, :] = tile.T

    def design_edges(h):
        some = pl.ds(h * half_rows, half_rows)
        return [
            remote(
                design.at[some, pl.ds(first, edge)], edge_design.at[side, some],
                edge_send.at[2 * h + side], edge_recv.at[2 * h + side], device,
            )
            for side, first, device in ((0, feats - edge, after), (1, 0, before))
        ]

    edges = (
        design_edges(0)
        + design_edges(1)
        + [
            remote(coef_two.at[pl.ds(feats - edge, edge)], edge_coef.at[0], edge_send.at[4], edge_recv.at[4], after),
            remote(coef_two.at[pl.ds(0, edge)], edge_coef.at[1], edge_send.at[5], edge_recv.at[5], before),
            remote(flags.at[pl.ds(0, 8)], flags.at[pl.ds(8, 8)], edge_send.at[6], edge_recv.at[6], after),
            remote(flags.at[pl.ds(0, 8)], flags.at[pl.ds(16, 8)], edge_send.at[7], edge_recv.at[7], before),
        ]
    )
    window = sorted([d for d in range(-REACH, REACH) if d], key=lambda d: -abs(d))
    across = sorted(range(NEAR, chips, NEAR), key=lambda d: -min(d, chips - d))

    for r in range(3):
        part[...] = fitted(1 - c)
        if r == 0:
            pl.semaphore_wait(barrier, NEAR + 2)
            hello(word.at[0], same(REACH))
            hello(word.at[0], same(-REACH))
        to_partner = remote(part, sent.at[r], pair_send.at[r], pair_recv.at[r], partner)
        to_partner.start()
        mine_half = fitted(c)
        if r == 0:
            pl.semaphore_wait(word.at[0], 2)
            hello(word.at[1], same(NEAR))
            hello(word.at[1], same(-NEAR))
        to_partner.wait_recv()
        half[...] = (mine_half + sent[r]).reshape(NEAR, piece, BLOCK)
        for d in window:
            remote(half.at[lax.rem(k + d + NEAR, NEAR)], near.at[r, d + REACH], near_send.at[r], near_recv.at[r], same(d)).start()
        drain(near.at[r, pl.ds(0, NEAR - 1)], near_recv.at[r])
        acc = half[k]
        for d in range(-REACH, REACH):
            if d:
                acc = acc + near[r, d + REACH]
        own[r] = acc
        far[r, block] = acc
        if r == 0:
            pl.semaphore_wait(word.at[1], 2)
        for d in across:
            remote(own.at[r], far.at[r, block], far_send.at[r], far_recv.at[r], same(d)).start()
        if r == 0:
            edges[6].start()
            edges[7].start()
            transpose_design()
        drain(far.at[r, pl.ds(0, blocks - 1)], far_recv.at[r])
        acc = far[r, 0]
        for j in range(1, blocks):
            acc = acc + far[r, j]
        acc = acc - tgt[c, k]
        total[r] = acc
        misfit[r, c, k] = acc
        for d in window:
            remote(total.at[r], misfit.at[r, c, k], all_send.at[r], all_recv.at[r], same(d)).start()
        drain(near.at[r, pl.ds(0, NEAR - 1)], all_recv.at[r])
        forward = remote(misfit.at[r, c], misfit.at[r, c], pass_send.at[r], pass_recv.at[r], partner)
        forward.start()
        if r:
            for e in edges[:2] if r == 1 else edges[2:6]:
                e.start()
        if r == 2:
            keep = pltpu.make_async_copy(coef_two, coef_home, load_sem.at[6 + CHUNKS])
            keep.start()
        for second in range(2):
            h = 1 - c if second else c
            if second:
                forward.wait_recv()
            high, low = halves(misfit[r, h].reshape(half_rows, BLOCK))
            pair = jnp.concatenate([high, low], axis=1)
            for i in range(CHUNKS):
                here = pl.ds(i * chunk, chunk)
                product = jnp.dot(cols[h, i], pair, preferred_element_type=f32)
                product = product[:chunk] + product[chunk:]
                product = product[:, :BLOCK] + product[:, BLOCK:]
                if not second:
                    corr[here, :] = product
                    continue
                product = product + corr[here, :]
                if r == 2:
                    top = jnp.max(jnp.abs(product), axis=0, keepdims=True)
                    peak = top if i == 0 else jnp.maximum(peak, top)
                    continue
                moved = point[here, :] - product * (1.0 / lipschitz)
                fresh = jnp.maximum(moved - level, 0.0) + jnp.minimum(moved + level, 0.0)
                if r == 0:
                    set_point(i, fresh + second_push * (fresh - cur[here, :]))
                else:
                    set_point(i, fresh)
                    coef_two[here, :] = fresh
                    mass = jnp.sum(jnp.abs(fresh), axis=0, keepdims=True)
                    local_mass = mass if i == 0 else local_mass + mass
        to_partner.wait_send()
        forward.wait_send()
        drain(near.at[r, pl.ds(0, NEAR - 1)], near_send.at[r])
        drain(far.at[r, pl.ds(0, blocks - 1)], far_send.at[r])
        drain(near.at[r, pl.ds(0, NEAR - 1)], all_send.at[r])

    upper = lax.broadcasted_iota(jnp.int32, (8, BLOCK), 0) < 4
    mine[...] = jnp.where(upper, jnp.broadcast_to(peak, (8, BLOCK)), jnp.broadcast_to(local_mass, (8, BLOCK)))
    swap = remote(mine, theirs, end_send.at[0], end_recv.at[0], partner)
    swap.start()
    swap.wait()
    joined = jnp.where(upper, jnp.maximum(mine[...], theirs[...]), mine[...] + theirs[...])
    both[...] = joined
    fin[0] = joined
    middle = chips // 2 + 1

    def exchange(first, last, sign, other_first, other_last):
        count = last - first

        @pl.loop(0, count)
        def _(i):
            slot = last - 1 - i if sign > 0 else first + i
            remote(both, fin.at[slot], end_send.at[1], end_recv.at[1], same(slot)).start()

        drain(fin.at[pl.ds(first, count)], end_recv.at[1])
        drain(fin.at[pl.ds(first, count)], end_send.at[1])
        out = remote(fin.at[pl.ds(first, count)], fin.at[pl.ds(first, count)], end_send.at[2], end_recv.at[2], partner)
        out.start()
        out.wait_send()
        drain(fin.at[pl.ds(other_first, other_last - other_first)], end_recv.at[2])

    @pl.when(c == 0)
    def _():
        exchange(1, middle, 1, middle, chips)

    @pl.when(c == 1)
    def _():
        exchange(middle, chips, -1, 1, middle)

    def gather(s, carry):
        tile = fin[lax.rem(z - s + chips, chips)]
        return jnp.maximum(carry[0], tile), carry[1] + tile

    zero = jnp.zeros((8, BLOCK), f32)
    most, sums = lax.fori_loop(0, chips, gather, (zero, zero))
    scale = jnp.maximum(pen[...], most[0:1] / samples)
    norm = sums[4:5]
    ratio = pen[...] / scale
    square = zero[0:1]
    for h in range(2):
        t = tgt[h].reshape(half_rows, BLOCK)
        res = -misfit[2, h].reshape(half_rows, BLOCK)
        dual = t - ratio * res
        parts = [jnp.sum(v * v, axis=0, keepdims=True) for v in (t, dual, res)]
        tsum, dsum, rsum = parts if h == 0 else [a + b for a, b in zip((tsum, dsum, rsum), parts)]
    dual_value = (tsum - dsum) / (2.0 * samples)
    gap = rsum / (2.0 * samples) + pen[...] * norm - dual_value
    stats[0:1, :] = gap
    stats[1:2, :] = dual_value
    stats[2:3, :] = norm
    stats[3:8, :] = jnp.zeros((5, BLOCK), f32)
    for e in edges:
        e.wait()
    keep.wait()


def place_kernel(
    flags_home, design, edge_design, coef, edge_coef, stats_home,
    coef_out, design_out, gap, dual_value, mass,
    flags, stats, tiles, coefs, blank, in_sem, coef_sem, out_sem, coef_out_sem, small_sem,
):
    slots = coefs.shape[0]
    feats = coef.shape[0]
    own = feats // BLOCK
    edge = own // 4
    me = lax.axis_index("feat")
    get_flags = pltpu.make_async_copy(flags_home, flags, small_sem.at[0])
    get_flags.start()
    get_stats = pltpu.make_async_copy(stats_home, stats, small_sem.at[1])
    get_stats.start()
    blank[...] = jnp.zeros_like(blank)
    get_flags.wait()

    def columns(j):
        return pl.ds(pl.multiple_of(j * BLOCK, BLOCK), BLOCK)

    slot = jnp.int32(0)
    places = []
    for cand in range(own + 2 * edge):
        if cand < edge:
            row, index = 8, own - edge + cand
        elif cand < edge + own:
            row, index = 0, cand - edge
        else:
            row, index = 16, cand - edge - own
        arrived = jnp.logical_and(flags[row, index] == 0, flags[row + 1, index] == me)
        places.append((arrived, slot))
        slot = slot + arrived.astype(jnp.int32)

    for cand, (arrived, where) in enumerate(places):
        if edge <= cand < edge + own:
            continue
        side, j = (0, cand) if cand < edge else (1, cand - edge - own)
        bank = side * edge + j

        @pl.when(arrived)
        def _():
            pltpu.make_async_copy(edge_design.at[side, :, columns(j)], tiles.at[bank], in_sem.at[bank]).start()
            pltpu.make_async_copy(edge_coef.at[side, columns(j), :], coefs.at[cand], coef_sem.at[cand]).start()

    for cand in range(edge, edge + own):
        arrived, where = places[cand]
        j = cand - edge

        @pl.when(arrived)
        def _():
            pltpu.make_async_copy(coef.at[columns(j), :], coefs.at[cand], coef_sem.at[cand]).start()
            pltpu.make_async_copy(design.at[:, columns(j)], design_out.at[:, columns(where)], out_sem).start()

    @pl.loop(slot, slots)
    def _(s):
        pltpu.make_async_copy(blank, design_out.at[:, columns(s)], out_sem).start()
        pltpu.make_async_copy(blank.at[pl.ds(0, BLOCK)], coef_out.at[columns(s), :], coef_out_sem).start()

    get_stats.wait()
    gap[...] = stats[0:1, :]
    dual_value[...] = stats[1:2, :]
    mass[...] = stats[2:3, :]
    for cand, (arrived, where) in enumerate(places):

        @pl.when(arrived)
        def _():
            if not edge <= cand < edge + own:
                bank = cand if cand < edge else cand - own
                pltpu.make_async_copy(tiles.at[bank], tiles.at[bank], in_sem.at[bank]).wait()
                pltpu.make_async_copy(tiles.at[bank], design_out.at[:, columns(where)], out_sem).start()
            pltpu.make_async_copy(coefs.at[cand], coefs.at[cand], coef_sem.at[cand]).wait()
            pltpu.make_async_copy(coefs.at[cand], coef_out.at[columns(where), :], coef_out_sem).start()

    pltpu.make_async_copy(design_out, design_out, out_sem).wait()
    pltpu.make_async_copy(coef_out, coef_out, coef_out_sem).wait()


def local(design, targets, coef_now, coef_prev, penalty, drop_mask, dest_shard):
    samples, feats = design.shape
    devices = lax.axis_size("feat")
    chips = devices // 2
    near, blocks = NEAR, chips // NEAR
    half_rows = samples // 2
    piece = half_rows // near
    chunk = feats // CHUNKS
    edge = feats // 4
    own = feats // BLOCK
    slots = own + own // 2
    anywhere = pl.BlockSpec(memory_space=pltpu.HBM)
    vector = pl.BlockSpec(memory_space=pltpu.VMEM)
    shape = jax.ShapeDtypeStruct
    dma = pltpu.SemaphoreType.DMA

    def home(x):
        return pltpu.with_memory_space_constraint(x, pltpu.HBM)

    def mem(*dims, dtype=f32):
        return pltpu.VMEM(dims, dtype)

    coef_two, edge_design, edge_coef, flags, stats = pl.pallas_call(
        fit_kernel,
        name="fit",
        out_shape=(
            shape((feats, BLOCK), f32),
            shape((2, samples, edge), f32),
            shape((2, edge, BLOCK), f32),
            shape((24, BLOCK), jnp.int32),
            shape((8, BLOCK), f32),
        ),
        in_specs=[anywhere] * 7,
        out_specs=(anywhere, anywhere, anywhere, vector, vector),
        scratch_shapes=[
            mem(feats, BLOCK), mem(samples, feats), mem(2, near, piece, BLOCK), mem(feats, BLOCK), mem(feats, BLOCK), mem(1, BLOCK),
            mem(1, own, dtype=jnp.int32), mem(1, own, dtype=jnp.int32),
            mem(2, samples, feats, dtype=bf16), mem(2, CHUNKS, 2 * chunk, half_rows, dtype=bf16),
            mem(feats, 2 * BLOCK, dtype=bf16), mem(feats, BLOCK), mem(feats, BLOCK),
            mem(half_rows, BLOCK), mem(near, piece, BLOCK), mem(3, half_rows, BLOCK), mem(3, near, piece, BLOCK),
            mem(3, piece, BLOCK), mem(3, blocks, piece, BLOCK), mem(3, piece, BLOCK), mem(3, 2, near, piece, BLOCK),
            mem(8, BLOCK), mem(8, BLOCK), mem(8, BLOCK), mem(chips, 8, BLOCK),
            dma((7 + CHUNKS,)),
        ]
        + [dma((3,))] * 10
        + [dma((8,))] * 2
        + [dma((3,))] * 2
        + [pltpu.SemaphoreType.REGULAR((2,))],
        compiler_params=pltpu.CompilerParams(collective_id=0, has_side_effects=True, vmem_limit_bytes=56 * 2**20),
        cost_estimate=pl.CostEstimate(flops=6 * 2 * samples * feats * BLOCK, bytes_accessed=8 * 2**20, transcendentals=0),
    )(
        design,
        targets.reshape(2, near, piece, BLOCK),
        coef_now,
        coef_prev,
        penalty.reshape(1, BLOCK),
        drop_mask.reshape(1, own),
        dest_shard.reshape(1, own),
    )
    coef_out, design_out, gap, dual_value, mass = pl.pallas_call(
        place_kernel,
        name="place",
        out_shape=(
            shape((slots * BLOCK, BLOCK), f32),
            shape((samples, slots * BLOCK), f32),
            shape((1, BLOCK), f32),
            shape((1, BLOCK), f32),
            shape((1, BLOCK), f32),
        ),
        in_specs=[anywhere, vector] + [anywhere] * 4,
        out_specs=(anywhere, anywhere, vector, vector, vector),
        scratch_shapes=[
            pltpu.SMEM((24, BLOCK), jnp.int32), mem(8, BLOCK), mem(own // 2, samples, BLOCK), mem(slots, BLOCK, BLOCK), mem(samples, BLOCK),
            dma((own // 2,)), dma((slots,)), dma, dma, dma((2,)),
        ],
        compiler_params=pltpu.CompilerParams(vmem_limit_bytes=24 * 2**20),
        cost_estimate=pl.CostEstimate(flops=2**20, bytes_accessed=15 * 2**20, transcendentals=0),
    )(home(flags), design, home(edge_design), home(coef_two), home(edge_coef), home(stats))
    return (coef_out, design_out, gap.reshape(BLOCK), dual_value.reshape(BLOCK), mass.reshape(BLOCK))


def solution(mesh):
    placed = (
        P("groups", "feat"),
        P("groups", None),
        P(("groups", "feat"), None),
        P(("groups", "feat"), None),
        P("groups"),
        P(("groups", "feat")),
        P(("groups", "feat")),
    )
    return jax.shard_map(
        local,
        mesh=mesh,
        in_specs=placed,
        out_specs=(
            P(("groups", "feat"), None),
            P("groups", "feat"),
            P("groups"),
            P("groups"),
            P("groups"),
        ),
        check_vma=False,
    )
```

time: 444 us -> 147 us (0.33)
  the two profiles are of different devices: /device:TPU:37 before, /device:TPU:101 now
where the time goes in v1:
time: 147 us; the launch traced here: 146 us
  Pallas kernels  146 us (99%)
    pallas_call x1, Pallas kernels, local(): pl.pallas_call(fit_kernel, name='fit', out_shape=(shape((feats, BLOCK), f...  140 us
    pallas_call x1, Pallas kernels, local(): pl.pallas_call(place_kernel, name='place', out_shape=(shape((slots * BLOC...  5.53 us

profile of v1, /device:TPU:101, one launch (start us, length us, event | category | flops | bytes accessed | tf_op | source)
XLA Modules:
  0.0 146.2 jit_solution(13416442682858365389)
XLA Ops:
  0.6 0.0 copy-start
  0.6 140.1 %fit.1 = (f32[2048,128]{1,0:T(8,128)}, f32[2,512,512]{2,1,0:T(8,128)}, f32[2,512,128]{2,1,0:T(8,128)}, s32[24,128]{1,0:T(8,128)}, f32[8,128]{1,0:T(8,128)}) custom-call(f32[512,2048]{1,0:T(8,128)} %design.3, f32[2,8,32,128]{3,2,1,0:T(8,128)} %bitcast.7, f32[2048,128]{1,0:T(8,128)} %now.1, f32[2048,128]{1,0:T(8,128)} %prev.1, f32[1,128]{1,0:T(1,128)} %bitcast.8, ...), custom_call_target="tpu_custom_call" | custom-call | flops 1610612736 | bytes 8388608 | tf_op jit(solution)/shard_map/fit/pallas_call | solution.py:399
  140.7 0.0 copy-done
  140.7 5.5 %place.1 = (f32[3072,128]{1,0:T(8,128)}, f32[512,3072]{1,0:T(8,128)}, f32[1,128]{1,0:T(1,128)}, f32[1,128]{1,0:T(1,128)}, f32[1,128]{1,0:T(1,128)}) custom-call(s32[24,128]{1,0:T(8,128)} %get-tuple-element.15.flags_home, f32[512,2048]{1,0:T(8,128)S(1)} %copy-done, f32[2,512,512]{2,1,0:T(8,128)} %get-tuple-element.16.edge_design, ...), custom_call_target="tpu_custom_call" | custom-call | flops 1048576 | bytes 15728640 | tf_op jit(solution)/shard_map/place/pallas_call | solution.py:436
Async XLA Ops:
  0.6 140.1 %copy-start = (f32[512,2048]{1,0:T(8,128)S(1)}, f32[512,2048]{1,0:T(8,128)}, u32[]{:S(2)}) copy-start(f32[512,2048]{1,0:T(8,128)} %design.3) | copy-start | bytes 12582916
